TPU v7x, 32 devices: a whole 2x2x4 slice. The times are simulated.
32 devices in a mesh: dp: 16 (over z, y, core), space: 2 (over x).
Axes of the slice: x: 2, y: 2, z: 4, core: 2. Of those that a mesh axis runs over, the one named last changes fastest.
Arguments:
- images: bfloat16 [16, 3, 512, 512], P('dp', None, 'space'), may hold values from -6 to 6
- pos_embed: bfloat16 [1024, 1280], P('space'), may hold values from -3 to 3
- conv_first: bfloat16 [3, 3, 3, 64], replicated, may hold values from -1.75 to 1.75
- conv_second: bfloat16 [3, 3, 64, 128], replicated, may hold values from -0.375 to 0.375
- conv_third: bfloat16 [3, 3, 128, 256], replicated, may hold values from -0.25 to 0.25
- conv_fourth: bfloat16 [3, 3, 256, 512], replicated, may hold values from -0.1875 to 0.1875
- proj_weight: bfloat16 [512, 1280], replicated, may hold values from -0.375 to 0.375
- ln_first: float32 [1280], replicated, may hold values from 0.25 to 1.75
- qkv_weight: bfloat16 [1280, 3, 1280], P('dp', None, 'space'), as said below
- out_weight: bfloat16 [1280, 1280], P('space', 'dp'), may hold values from -0.15625 to 0.15625
- ln_second: float32 [1280], replicated, may hold values from 0.25 to 1.75
- up_weight: bfloat16 [1280, 5120], P('dp', 'space'), may hold values from -0.15625 to 0.15625
- down_weight: bfloat16 [5120, 1280], P('space', 'dp'), may hold values from -0.125 to 0.125
Outputs:
- encoded: bfloat16 [16, 1024, 1280], P('dp', 'space')
Inputs may be any that keep to these rules, and one draw needn't show every extreme that they name: `qkv_weight`: every entry is at most 135 * 1280 ** -0.5 in magnitude.
All inputs are finite; a program needn't handle non-finite values.
Results may differ from a plain program's by a relative error of at most 0.014.
Values may be sent and summed in bfloat16 or wider, within the bound.
A program may use at most 128 MiB of HBM per device.

v0:
```python
import jax
import jax.numpy as jnp
from jax import lax
from jax.sharding import PartitionSpec as P

HEADS = 16


def passed_along(value, axis, steps):
    count = lax.axis_size(axis)
    leading, last = (max(0, -steps), min(count, count - steps))
    return lax.ppermute(value, axis, [(source, source + steps) for source in range(leading, last)])


def conv_rows(image_field, kernel, spec):
    out = lax.conv_general_dilated(
        image_field,
        kernel,
        (2, 2),
        ((0, 0), (1, 1)),
        dimension_numbers=spec,
        preferred_element_type=jnp.float32,
    )
    return jax.nn.relu(out).astype(jnp.bfloat16)


def layer_norm(values, gain):
    wide = values.astype(jnp.float32)
    center = wide - jnp.mean(wide, axis=-1, keepdims=True)
    spread = jnp.mean(center * center, axis=-1, keepdims=True)
    return (center * lax.rsqrt(spread + 1e-06) * gain).astype(jnp.bfloat16)


def attend(query, keys, values):
    head_size = query.shape[-1]
    divisor = jnp.sqrt(jnp.float32(head_size))

    def one_head(items):
        head_query, head_keys, head_values = items
        scores = (
            jnp.einsum("gqd,gkd->gqk", head_query, head_keys, preferred_element_type=jnp.float32)
            / divisor
        )
        weights = jax.nn.softmax(scores, axis=-1).astype(jnp.bfloat16)
        return jnp.einsum(
            "gqk,gkd->gqd", weights, head_values, preferred_element_type=jnp.float32
        ).astype(jnp.bfloat16)

    mixed = lax.map(
        one_head, (jnp.moveaxis(query, 2, 0), jnp.moveaxis(keys, 2, 0), jnp.moveaxis(values, 2, 0))
    )
    return jnp.moveaxis(mixed, 0, 2)


def device_rows(values, start, total, groups, per_device, weight):
    token_start = start // groups
    token_count = total // groups
    slab = lax.dynamic_slice_in_dim(values, token_start, token_count, 1)
    owners = token_count // per_device
    slab = slab.reshape(groups, owners, per_device, values.shape[2])
    slab = jnp.transpose(slab, (1, 0, 2, 3)).reshape(total, values.shape[2])
    return jnp.dot(slab, weight, preferred_element_type=jnp.float32)


def on_device(
    images,
    pos_embed,
    conv_first,
    conv_second,
    conv_third,
    conv_fourth,
    proj_weight,
    ln_first,
    qkv_weight,
    out_weight,
    ln_second,
    up_weight,
    down_weight,
):
    spec_first = ("NCHW", "HWIO", "NHWC")
    spec_later = ("NHWC", "HWIO", "NHWC")
    margin = passed_along(images[:, :, -15:, :], "space", 1)
    stem_out = conv_rows(jnp.concatenate([margin, images], axis=2), conv_first, spec_first)
    for kernel in (conv_second, conv_third, conv_fourth):
        stem_out = conv_rows(stem_out, kernel, spec_later)
    groups, height, across, channels = stem_out.shape
    flat = stem_out.reshape(groups, height * across, channels)
    tokens = (
        jnp.dot(flat, proj_weight, preferred_element_type=jnp.float32)
        + pos_embed.astype(jnp.float32)
    ).astype(jnp.bfloat16)
    qkv_part, out_part = (
        lax.all_gather(qkv_weight, "dp", axis=0, tiled=True),
        lax.all_gather(out_weight, "dp", axis=1, tiled=True),
    )
    width = tokens.shape[2]
    count = tokens.shape[1]
    local = qkv_part.shape[2]
    head_size = width // HEADS
    local_heads = local // head_size
    qkv_matrix = qkv_part.reshape(width, 3 * local)
    qkv_all = jnp.dot(
        layer_norm(lax.all_gather(tokens, "space", axis=1, tiled=True), ln_first),
        qkv_matrix,
        preferred_element_type=jnp.float32,
    ).astype(jnp.bfloat16)
    seen = qkv_all.shape[1]
    qkv_all = qkv_all.reshape(groups, seen, 3, local_heads, head_size)
    mixed = attend(qkv_all[:, :, 0], qkv_all[:, :, 1], qkv_all[:, :, 2]).reshape(
        groups, seen, local
    )
    attn_sum = (
        lax.psum_scatter(
            device_rows(
                mixed,
                jnp.int32(0),
                groups * count * lax.axis_size("space"),
                groups,
                count,
                out_part,
            ).astype(jnp.bfloat16),
            "space",
            scatter_dimension=0,
            tiled=True,
        )
        .astype(jnp.float32)
        .reshape(groups, count, width)
    )
    after_attn = (tokens.astype(jnp.float32) + attn_sum).astype(jnp.bfloat16)
    normed_two = layer_norm(after_attn, ln_second)
    group_rows = lax.all_gather(normed_two, "space", axis=1, tiled=True)
    seen_rows = group_rows.shape[1]
    hidden_cols = up_weight.shape[1]
    start_hidden = jnp.zeros((groups, seen_rows, hidden_cols), jnp.float32)
    before_gelu = start_hidden + jnp.einsum(
        "gtd,df->gtf",
        group_rows,
        lax.all_gather(up_weight, "dp", axis=0, tiled=True),
        preferred_element_type=jnp.float32,
    )
    hidden = jax.nn.gelu(before_gelu, approximate=False).astype(jnp.bfloat16)
    down_part = lax.all_gather(down_weight, "dp", axis=1, tiled=True)
    mlp_sum = (
        lax.psum_scatter(
            device_rows(
                hidden,
                jnp.int32(0),
                groups * count * lax.axis_size("space"),
                groups,
                count,
                down_part,
            ).astype(jnp.bfloat16),
            "space",
            scatter_dimension=0,
            tiled=True,
        )
        .astype(jnp.float32)
        .reshape(groups, count, width)
    )
    return (after_attn.astype(jnp.float32) + mlp_sum).astype(jnp.bfloat16)


def solution(mesh):
    placed = (
        P("dp", None, "space", None),
        P("space", None),
        P(),
        P(),
        P(),
        P(),
        P(),
        P(),
        P("dp", None, "space"),
        P("space", "dp"),
        P(),
        P("dp", "space"),
        P("space", "dp"),
    )
    return jax.shard_map(
        on_device, mesh=mesh, in_specs=placed, out_specs=P("dp", "space", None), check_vma=False
    )
```

profile of v0, /device:TPU:0, one launch (start us, length us, event | category | flops | bytes accessed | tf_op | source)
XLA Modules:
  0.0 586.7 jit_solution(12435895969867735964)
XLA Ops:
  7.5 4.9 collective-permute-start
  15.9 2.9 reshape.228
  18.8 19.6 %copy.46 = bf16[3,271,1,8,66]{3,0,4,1,2:T(4,128)(2,1)} copy(bf16[3,271,1,8,66]{4,3,1,0,2:T(8,128)(2,1)} %reshape.228) | data formatting | bytes 1717056 | tf_op jit(solution)/shard_map/conv_general_dilated | solution.py:16
  39.8 27.8 %fusion.44 = bf16[135,8,33,64]{3,1,2,0:T(8,128)(2,1)} fusion(pred[8,33]{0,1:T(8,128)(4,1)S(1)} %copy-done.8, bf16[3,3,3,64]{3,2,1,0:T(4,128)(2,1)S(1)} %copy-done.6, bf16[3,271,1,7,2]{3,0,4,1,2:T(4,128)(2,1)S(1)} %slice.25, bf16[3,271,1,8,66]{3,0,4,1,2:T(4,128)(2,1)} %copy.46), kind=kOutput, calls=%fused_computation.57 | convolution fusion | flops 134949312 | bytes 5446932 | tf_op jit(solution)/shard_map/conv_general_dilated | solution.py:16
  67.6 16.3 %copy.47 = bf16[135,8,33,64]{0,3,2,1:T(8,128)(2,1)} copy(bf16[135,8,33,64]{3,1,2,0:T(8,128)(2,1)} %fusion.44) | data formatting | bytes 9123840 | tf_op jit(solution)/shard_map/convert_element_type | solution.py:24
  84.0 8.3 %slice.26 = bf16[135,1,256,64]{0,3,2,1:T(8,128)(2,1)} slice(bf16[135,1,264,64]{0,3,2,1:T(8,128)(2,1)} %bitcast.122), slice={[0:135], [0:1], [0:256], [0:64]} | slice | bytes 8847360 | tf_op jit(solution)/shard_map/convert_element_type | solution.py:24
  92.3 15.6 %copy.48 = bf16[135,1,8,32,64]{4,2,3,0,1:T(8,128)(2,1)} copy(bf16[135,1,8,32,64]{0,4,3,2,1:T(8,128)(2,1)} %bitcast.123) | data formatting | bytes 8847360 | tf_op jit(solution)/shard_map/convert_element_type | solution.py:24
  109.1 6.6 %fusion.86 = bf16[67,1,8,16,128]{4,2,3,0,1:T(8,128)(2,1)S(1)} fusion(bf16[3,3,64,128]{3,2,1,0:T(8,128)(2,1)S(1)} %copy-done.5, bf16[135,1,7,1,64]{4,2,3,0,1:T(8,128)(2,1)S(1)} %get-tuple-element.63, bf16[135,1,7,1,64]{4,2,3,0,1:T(8,128)(2,1)S(1)} %get-tuple-element.62, bf16[135,1,8,32,64]{4,2,3,0,1:T(8,128)(2,1)} %copy.48), kind=kOutput, calls=%fused_computation.105 | convolution fusion | flops 1290278912 | bytes 7008512 | tf_op jit(solution)/shard_map/conv_general_dilated | solution.py:16
  119.3 3.7 fusion.63
  124.5 39.7 %all-gather.17.cloned.1.call-done = bf16[1024,1280]{1,0:T(8,128)(2,1)} async-done(((bf16[512,1280]{1,0:T(8,128)(2,1)}), bf16[1024,1280]{1,0:T(8,128)(2,1)}) %all-gather.17.cloned.1.call-update) | async-done | bytes 2621456 | tf_op jit(solution)/shard_map/all_gather | solution.py:103
  166.4 2.6 fusion.50
  169.0 51.6 %all-gather.9.cloned.1.call-done = bf16[1280,3,640]{2,0,1:T(8,128)(2,1)} async-done(((bf16[80,3,640]{2,0,1:T(8,128)(2,1)}), bf16[1280,3,640]{2,0,1:T(8,128)(2,1)}) %all-gather.9.cloned.1.call-update) | async-done | bytes 4915216 | tf_op jit(solution)/shard_map/all_gather | solution.py:93
  220.6 8.2 %copy.52 = bf16[1280,3,640]{0,2,1:T(8,128)(2,1)} copy(bf16[1280,3,640]{2,0,1:T(8,128)(2,1)} %all-gather.9.cloned.1.call-done) | data formatting | bytes 9830400 | tf_op jit(solution)/shard_map/all_gather | solution.py:93
  228.8 10.3 %convolution_convert_fusion.1 = bf16[1024,1920]{1,0:T(8,128)(2,1)} fusion(bf16[1280,1920]{0,1:T(8,128)(2,1)} %bitcast.125, bf16[1024,1280]{1,0:T(8,128)(2,1)} %all-gather.17.cloned.1.call-done, f32[1280]{0:T(1024)S(1)} %copy-done.7, f32[1024]{0:T(1024)S(1)} %add_rsqrt_fusion, f32[1024]{0:T(1024)S(1)} %broadcast_multiply_fusion), kind=kOutput, calls=%fused_computation.78 | convolution fusion | flops 5041684480 | bytes 11482112 | tf_op jit(solution)/shard_map/dot_general | solution.py:102
  239.0 6.3 %copy.53 = bf16[1024,1920]{0,1:T(8,128)(2,1)} copy(bf16[1024,1920]{1,0:T(8,128)(2,1)} %convolution_convert_fusion.1) | data formatting | bytes 7864320 | tf_op jit(solution)/shard_map/convert_element_type | solution.py:106
  245.3 4.2 slice_bitcast_fusion
  249.5 39.8 %while.10 = (s32[]{:T(128)}, bf16[8,1,1024,80]{2,3,1,0:T(8,128)(2,1)}, bf16[8,1,1024,80]{2,3,0,1:T(8,128)(2,1)}, bf16[8,1,1024,80]{2,3,0,1:T(8,128)(2,1)S(1)}, bf16[8,1,1024,80]{2,3,0,1:T(8,128)(2,1)}, /*index=5*/s32[]{:T(128)}) while((s32[]{:T(128)}, bf16[8,1,1024,80]{2,3,1,0:T(8,128)(2,1)}, bf16[8,1,1024,80]{2,3,0,1:T(8,128)(2,1)}, ...), condition=%wide.region_5.6_spmd, body=%wide.region_2.5_spmd.sunk | while | flops 345061376 | bytes 13260869 | solution.py:49
  256.9 2.6 fusion.187
  261.9 2.6 fusion.187
  266.9 2.6 fusion.187
  271.9 2.6 fusion.187
  276.9 2.6 fusion.187
  281.8 2.6 fusion.187
  286.8 2.6 fusion.187
  289.4 5.5 convolution_convert_fusion
  296.2 35.4 %reduce-scatter.3.cloned.1.call-done = bf16[512,1280]{1,0:T(8,128)(2,1)} async-done(((bf16[1024,1280]{1,0:T(8,128)(2,1)}), bf16[512,1280]{1,0:T(8,128)(2,1)}) %reduce-scatter.3.cloned.1.call-update) | async-done | bytes 1310736 | tf_op jit(solution)/shard_map/reduce_scatter | solution.py:113
  336.4 60.2 %all-gather.13.cloned.1.call-done = bf16[1280,2560]{1,0:T(8,128)(2,1)} async-done(((bf16[80,2560]{1,0:T(8,128)(2,1)}), bf16[1280,2560]{1,0:T(8,128)(2,1)}) %all-gather.13.cloned.1.call-update) | async-done | bytes 6553616 | tf_op jit(solution)/shard_map/all_gather | solution.py:138
  396.6 63.7 %all-gather.15.cloned.1.call-done = bf16[2560,1280]{0,1:T(8,128)(2,1)} async-done(((bf16[2560,80]{0,1:T(8,128)(2,1)}), bf16[2560,1280]{0,1:T(8,128)(2,1)}) %all-gather.15.cloned.1.call-update) | async-done | bytes 6553616 | tf_op jit(solution)/shard_map/all_gather | solution.py:142
  460.3 39.3 %all-gather.19.cloned.1.call-done = bf16[1024,1280]{1,0:T(8,128)(2,1)} async-done(((bf16[512,1280]{1,0:T(8,128)(2,1)}), bf16[1024,1280]{1,0:T(8,128)(2,1)}) %all-gather.19.cloned.1.call-update) | async-done | bytes 2621456 | tf_op jit(solution)/shard_map/all_gather | solution.py:131
  499.6 38.9 %fusion.58 = bf16[1024,1280]{1,0:T(8,128)(2,1)} fusion(bf16[2560,1280]{0,1:T(8,128)(2,1)} %all-gather.15.cloned.1.call-done, bf16[1024,1280]{1,0:T(8,128)(2,1)} %all-gather.19.cloned.1.call-done, bf16[1280,2560]{1,0:T(8,128)(2,1)} %all-gather.13.cloned.1.call-done), kind=kOutput, calls=%fused_computation.76 | convolution fusion | flops 13593477120 | bytes 18350080 | tf_op jit(solution)/shard_map/dot_general | solution.py:62
  538.5 37.8 %reduce-scatter.5.cloned.1.call-done = bf16[512,1280]{1,0:T(8,128)(2,1)} async-done(((bf16[1024,1280]{1,0:T(8,128)(2,1)}), bf16[512,1280]{1,0:T(8,128)(2,1)}) %reduce-scatter.5.cloned.1.call-update) | async-done | bytes 1310736 | tf_op jit(solution)/shard_map/reduce_scatter | solution.py:144
  576.4 3.1 fusion.104
  (73 shorter events, 42.1 us)
Async XLA Ops:
  6.5 110.9 %copy-start = (bf16[3,3,256,512]{3,2,1,0:T(8,128)(2,1)S(1)}, bf16[3,3,256,512]{3,2,1,0:T(8,128)(2,1)}, u32[]{:S(2)}) copy-start(bf16[3,3,256,512]{3,2,1,0:T(8,128)(2,1)} %param.20) | copy-start | bytes 7077892
  6.5 157.7 %all-gather.17.cloned.1.call-start = ((), (), s32[]{:S(2)}) async-start(), calls=%async_computation.8 | async-start | bytes 3932160 | tf_op jit(solution)/shard_map/all_gather | solution.py:103
  7.5 6.6 %collective-permute-start = (bf16[1,3,15,512]{3,2,1,0:T(8,128)(2,1)S(1)}, bf16[1,3,15,512]{3,2,1,0:T(8,128)(2,1)S(1)}, u32[]{:S(2)}, u32[]{:S(2)}) collective-permute-start(bf16[1,3,15,512]{3,2,1,0:T(8,128)(2,1)S(1)} %slice.12), channel_id=1, source_target_pairs={{0,1},{2,3},{4,5},{6,7},{8,9},{10,11},{12,13},{14,15},{16,17},{18,... | collective-permute-start | bytes 138248 | tf_op jit(solution)/shard_map/ppermute | solution.py:12
  18.8 21.0 %copy-start.6 = (bf16[3,3,3,64]{3,2,1,0:T(4,128)(2,1)S(1)}, bf16[3,3,3,64]{3,2,1,0:T(4,128)(2,1)}, u32[]{:S(2)}) copy-start(bf16[3,3,3,64]{3,2,1,0:T(4,128)(2,1)} %param.17) | copy-start | bytes 10372
  18.8 21.0 %copy-start.8 = (pred[8,33]{0,1:T(8,128)(4,1)S(1)}, pred[8,33]{0,1:T(8,128)(4,1)}, u32[]{:S(2)}) copy-start(pred[8,33]{0,1:T(8,128)(4,1)} %constant.128) | copy-start | bytes 796
  92.3 16.8 %copy-start.5 = (bf16[3,3,64,128]{3,2,1,0:T(8,128)(2,1)S(1)}, bf16[3,3,64,128]{3,2,1,0:T(8,128)(2,1)}, u32[]{:S(2)}) copy-start(bf16[3,3,64,128]{3,2,1,0:T(8,128)(2,1)} %param.18) | copy-start | bytes 442372
  109.1 6.7 %copy-start.4 = (bf16[3,3,128,256]{3,2,1,0:T(8,128)(2,1)S(1)}, bf16[3,3,128,256]{3,2,1,0:T(8,128)(2,1)}, u32[]{:S(2)}) copy-start(bf16[3,3,128,256]{3,2,1,0:T(8,128)(2,1)} %param.19) | copy-start | bytes 1769476
  123.0 97.6 %all-gather.9.cloned.1.call-start = ((), (), s32[]{:S(2)}) async-start(), calls=%async_computation.2 | async-start | bytes 5222400 | tf_op jit(solution)/shard_map/all_gather | solution.py:93
  123.7 165.7 %all-gather.11.cloned.1.call-start = ((), (), s32[]{:S(2)}) async-start(), calls=%async_computation.3 | async-start | bytes 1740800 | tf_op jit(solution)/shard_map/all_gather | solution.py:94
  124.5 207.1 %reduce-scatter.3.cloned.1.call-start = ((), (), s32[]{:S(2)}) async-start(), calls=%async_computation.4 | async-start | bytes 3932160 | tf_op jit(solution)/shard_map/reduce_scatter | solution.py:113
  169.0 59.8 %copy-start.7 = (f32[1280]{0:T(1024)S(1)}, f32[1280]{0:T(1024)}, u32[]{:S(2)}) copy-start(f32[1280]{0:T(1024)} %param.22) | copy-start | bytes 15364
  294.9 39.9 %copy-start.3 = (f32[1280]{0:T(1024)S(1)}, f32[1280]{0:T(1024)}, u32[]{:S(2)}) copy-start(f32[1280]{0:T(1024)} %param.25) | copy-start | bytes 15364
  295.0 101.6 %all-gather.13.cloned.1.call-start = ((), (), s32[]{:S(2)}) async-start(), calls=%async_computation.5 | async-start | bytes 6963200 | tf_op jit(solution)/shard_map/all_gather | solution.py:138
  295.5 164.8 %all-gather.15.cloned.1.call-start = ((), (), s32[]{:S(2)}) async-start(), calls=%async_computation.6 | async-start | bytes 6963200 | tf_op jit(solution)/shard_map/all_gather | solution.py:142
  296.1 203.5 %all-gather.19.cloned.1.call-start = ((), (), s32[]{:S(2)}) async-start(), calls=%async_computation.9 | async-start | bytes 3932160 | tf_op jit(solution)/shard_map/all_gather | solution.py:131
  333.7 1.1 copy-start.2
  336.3 240.1 %reduce-scatter.5.cloned.1.call-start = ((), (), s32[]{:S(2)}) async-start(), calls=%async_computation.7 | async-start | bytes 3932160 | tf_op jit(solution)/shard_map/reduce_scatter | solution.py:144
  499.6 79.8 %copy-start.1 = (bf16[3,3,256,512]{3,2,1,0:T(8,128)(2,1)S(1)}, bf16[3,3,256,512]{3,2,1,0:T(8,128)(2,1)}, u32[]{:S(2)}) copy-start(bf16[3,3,256,512]{3,2,1,0:T(8,128)(2,1)} %param.20) | copy-start | bytes 7077892
Sparse Core Ops, SparseCore 0:
  123.1 41.0 all-gather.16
  166.4 54.1 all-gather.8
  222.8 38.4 all-gather.10
  295.1 36.4 reduce-scatter.2
  333.7 62.8 all-gather.12
  398.7 61.5 all-gather.14
  461.9 37.7 all-gather.18
  538.7 37.6 reduce-scatter.4
where the time goes:
time: 598 us; the launch traced here: 587 us
  waiting for transfers between devices  332 us (56%)
  matrix products  130 us (22%)
  local copies, waits for them, and re-layouts  86.5 us (14%)
  other arithmetic  19.2 us (3%)
  between operations  14.1 us (2%)
    all_gather x1, waiting for transfers between devices, on_device(): down_part = lax.all_gather(down_weight, 'dp', axis=1, tiled=True)  63.7 us
    all_gather x1, waiting for transfers between devices, on_device(): lax.all_gather(up_weight, 'dp', axis=0, tiled=True)  60.2 us
    all_gather x1, waiting for transfers between devices, on_device(): lax.all_gather(qkv_weight, 'dp', axis=0, tiled=True)  51.6 us
    dot_general x2, matrix products, device_rows(): return jnp.dot(slab, weight, preferred_element_type=jnp.float32)  44.5 us
    convert_element_type x7, local copies, waits for them, and re-layouts, conv_rows(): return jax.nn.relu(out).astype(jnp.bfloat16)  41.8 us
    all_gather x1, waiting for transfers between devices, on_device(): lax.all_gather(tokens, 'space', axis=1, tiled=True)  39.7 us
    all_gather x1, waiting for transfers between devices, on_device(): group_rows = lax.all_gather(normed_two, 'space', axis=1, tiled=True)  39.3 us
    reduce_scatter x1, waiting for transfers between devices, on_device(): lax.psum_scatter(device_rows(hidden, jnp.int32(0), groups * count * lax.a...  37.8 us
  transfers between devices with their start and end apart: 9, of which 8 were waited for; matrix products, arithmetic and copies ran while one was open for 13% of the time, Pallas kernels for 0%

commit v1 on v0

--- a/solution.py
+++ b/solution.py
@@ -139,7 +139,12 @@
         preferred_element_type=jnp.float32,
     )
     hidden = jax.nn.gelu(before_gelu, approximate=False).astype(jnp.bfloat16)
-    down_part = lax.all_gather(down_weight, "dp", axis=1, tiled=True)
+    ring = [down_weight]
+    for hop in range(15):
+        ring.append(lax.ppermute(ring[-1], "dp", [(dev, (dev + 1) % 16) for dev in range(16)]))
+    down_part = jnp.roll(
+        jnp.concatenate(ring[::-1], axis=1), (lax.axis_index("dp") + 1) * ring[0].shape[1], axis=1
+    )
     mlp_sum = (
         lax.psum_scatter(
             device_rows(

time: 598 us -> 660 us (1.10)
  local copies, waits for them, and re-layouts: 86.5 us -> 133 us
  matrix products: 130 us -> 142 us
    ppermute x0 -> x15, waiting for transfers between devices: none -> 176 us  [on_device(): lax.ppermute(ring[-1], 'dp', [(dev, (dev + 1) % 16) for dev in range(16)])]
    all_gather x1 -> x0, waiting for transfers between devices: 63.7 us -> none  [on_device(): down_part = lax.all_gather(down_weight, 'dp', axis=1, tiled=True)]
    all_gather x1, waiting for transfers between devices: 60.2 us -> 0.01 us  [on_device(): lax.all_gather(up_weight, 'dp', axis=0, tiled=True)]
    unnamed x18 -> x75, local copies, waits for them, and re-layouts: 0.6 us -> 46.1 us
    reduce_scatter x1, waiting for transfers between devices: 35.4 us -> 0.01 us  [on_device(): lax.psum_scatter(device_rows(mixed, jnp.int32(0), groups * count * lax.ax...]
    all_gather x1, waiting for transfers between devices: 39.3 us -> 25.9 us  [on_device(): group_rows = lax.all_gather(normed_two, 'space', axis=1, tiled=True)]
    conv_general_dilated x4, matrix products: 37.5 us -> 49.4 us  [conv_rows(): lax.conv_general_dilated(image_field, kernel, (2, 2), ((0, 0), (1, 1)), d...]
  transfers between devices with their start and end apart: 9 -> 23, of which waited for: 8 -> 20; matrix products, arithmetic and copies ran while one was open for 13% -> 19% of each run, Pallas kernels for 0% -> 0%
where the time goes in v1:
time: 660 us; the launch traced here: 648 us
  waiting for transfers between devices  334 us (51%)
  matrix products  142 us (22%)
  local copies, waits for them, and re-layouts  133 us (20%)
  other arithmetic  19.2 us (3%)
  between operations  14.1 us (2%)
    ppermute x15, waiting for transfers between devices, on_device(): lax.ppermute(ring[-1], 'dp', [(dev, (dev + 1) % 16) for dev in range(16)])  176 us
    all_gather x1, waiting for transfers between devices, on_device(): lax.all_gather(qkv_weight, 'dp', axis=0, tiled=True)  51.6 us
    conv_general_dilated x4, matrix products, conv_rows(): lax.conv_general_dilated(image_field, kernel, (2, 2), ((0, 0), (1, 1)), d...  49.4 us
    unnamed x75, local copies, waits for them, and re-layouts  46.1 us
    dot_general x2, matrix products, device_rows(): return jnp.dot(slab, weight, preferred_element_type=jnp.float32)  45.2 us
    convert_element_type x7, local copies, waits for them, and re-layouts, conv_rows(): return jax.nn.relu(out).astype(jnp.bfloat16)  41.9 us
    all_gather x1, waiting for transfers between devices, on_device(): lax.all_gather(tokens, 'space', axis=1, tiled=True)  39.7 us
    reduce_scatter x1, waiting for transfers between devices, on_device(): lax.psum_scatter(device_rows(hidden, jnp.int32(0), groups * count * lax.a...  37.8 us
  transfers between devices with their start and end apart: 23, of which 20 were waited for; matrix products, arithmetic and copies ran while one was open for 19% of the time, Pallas kernels for 0%

profile of v1, /device:TPU:0, one launch (start us, length us, event | category | flops | bytes accessed | tf_op | source)
XLA Modules:
  0.0 648.1 jit_solution(9700133494078263349)
XLA Ops:
  7.5 4.9 collective-permute-start
  18.8 19.6 %copy.46 = bf16[3,271,1,8,66]{3,0,4,1,2:T(4,128)(2,1)} copy(bf16[3,271,1,8,66]{4,3,1,0,2:T(8,128)(2,1)} %reshape.228) | data formatting | bytes 1717056 | tf_op jit(solution)/shard_map/conv_general_dilated | solution.py:16
  39.9 27.8 %fusion.44 = bf16[135,8,33,64]{3,1,2,0:T(8,128)(2,1)} fusion(pred[8,33]{0,1:T(8,128)(4,1)S(1)} %copy-done.21, bf16[3,3,3,64]{3,2,1,0:T(4,128)(2,1)S(1)} %copy-done.19, bf16[3,271,1,7,2]{3,0,4,1,2:T(4,128)(2,1)S(1)} %slice.25, bf16[3,271,1,8,66]{3,0,4,1,2:T(4,128)(2,1)} %copy.46), kind=kOutput, calls=%fused_computation.57 | convolution fusion | flops 134949312 | bytes 5446932 | tf_op jit(solution)/shard_map/conv_general_dilated | solution.py:16
  67.7 16.4 %copy.47 = bf16[135,8,33,64]{0,3,2,1:T(8,128)(2,1)} copy(bf16[135,8,33,64]{3,1,2,0:T(8,128)(2,1)} %fusion.44) | data formatting | bytes 9123840 | tf_op jit(solution)/shard_map/convert_element_type | solution.py:24
  84.1 8.3 %slice.26 = bf16[135,1,256,64]{0,3,2,1:T(8,128)(2,1)} slice(bf16[135,1,264,64]{0,3,2,1:T(8,128)(2,1)} %bitcast.113), slice={[0:135], [0:1], [0:256], [0:64]} | slice | bytes 8847360 | tf_op jit(solution)/shard_map/convert_element_type | solution.py:24
  92.4 15.6 %copy.48 = bf16[135,1,8,32,64]{4,2,3,0,1:T(8,128)(2,1)} copy(bf16[135,1,8,32,64]{0,4,3,2,1:T(8,128)(2,1)} %bitcast.114) | data formatting | bytes 8847360 | tf_op jit(solution)/shard_map/convert_element_type | solution.py:24
  109.2 18.6 %fusion.118 = bf16[67,1,8,16,128]{4,2,3,0,1:T(8,128)(2,1)S(1)} fusion(bf16[3,3,64,128]{3,2,1,0:T(8,128)(2,1)S(1)} %copy-done.18, bf16[135,1,7,1,64]{4,2,3,0,1:T(8,128)(2,1)S(1)} %get-tuple-element.63, bf16[135,1,7,1,64]{4,2,3,0,1:T(8,128)(2,1)S(1)} %get-tuple-element.62, bf16[135,1,8,32,64]{4,2,3,0,1:T(8,128)(2,1)} %copy.48), kind=kOutput, calls=%fused_computation.135 | convolution fusion | flops 1290278912 | bytes 7008512 | tf_op jit(solution)/shard_map/conv_general_dilated | solution.py:16
  136.6 39.7 %all-gather.14.cloned.1.call-done = bf16[1024,1280]{1,0:T(8,128)(2,1)} async-done(((bf16[512,1280]{1,0:T(8,128)(2,1)}), bf16[1024,1280]{1,0:T(8,128)(2,1)}) %all-gather.14.cloned.1.call-update) | async-done | bytes 2621456 | tf_op jit(solution)/shard_map/all_gather | solution.py:103
  181.0 51.6 %all-gather.8.cloned.1.call-done = bf16[1280,3,640]{2,0,1:T(8,128)(2,1)} async-done(((bf16[80,3,640]{2,0,1:T(8,128)(2,1)}), bf16[1280,3,640]{2,0,1:T(8,128)(2,1)}) %all-gather.8.cloned.1.call-update) | async-done | bytes 4915216 | tf_op jit(solution)/shard_map/all_gather | solution.py:93
  232.6 8.2 %copy.52 = bf16[1280,3,640]{0,2,1:T(8,128)(2,1)} copy(bf16[1280,3,640]{2,0,1:T(8,128)(2,1)} %all-gather.8.cloned.1.call-done) | data formatting | bytes 9830400 | tf_op jit(solution)/shard_map/all_gather | solution.py:93
  240.8 10.4 %convolution_convert_fusion.1 = bf16[1024,1920]{1,0:T(8,128)(2,1)} fusion(bf16[1280,1920]{0,1:T(8,128)(2,1)} %bitcast.116, bf16[1024,1280]{1,0:T(8,128)(2,1)} %all-gather.14.cloned.1.call-done, f32[1280]{0:T(1024)S(1)} %copy-done.20, f32[1024]{0:T(1024)S(1)} %add_rsqrt_fusion, f32[1024]{0:T(1024)S(1)} %broadcast_multiply_fusion), kind=kOutput, calls=%fused_computation.108 | convolution fusion | flops 5041684480 | bytes 11482112 | tf_op jit(solution)/shard_map/dot_general | solution.py:102
  251.2 6.3 copy.53
  261.7 39.8 %while.10 = (s32[]{:T(128)}, bf16[8,1,1024,80]{2,3,1,0:T(8,128)(2,1)}, bf16[8,1,1024,80]{2,3,0,1:T(8,128)(2,1)}, bf16[8,1,1024,80]{2,3,0,1:T(8,128)(2,1)S(1)}, bf16[8,1,1024,80]{2,3,0,1:T(8,128)(2,1)}, /*index=5*/s32[]{:T(128)}) while((s32[]{:T(128)}, bf16[8,1,1024,80]{2,3,1,0:T(8,128)(2,1)}, bf16[8,1,1024,80]{2,3,0,1:T(8,128)(2,1)}, ...), condition=%wide.region_5.6_spmd, body=%wide.region_2.5_spmd.sunk | while | flops 345061376 | bytes 13260869 | solution.py:49
  301.5 5.7 convolution_convert_fusion
  307.6 9.8 %collective-permute-done.1 = bf16[2560,80]{0,1:T(8,128)(2,1)S(1)} collective-permute-done((bf16[2560,80]{0,1:T(8,128)(2,1)S(1)}, bf16[2560,80]{0,1:T(8,128)(2,1)S(1)}, u32[]{:S(2)}, u32[]{:S(2)}) %collective-permute-start.1) | collective-permute-done | bytes 409632 | tf_op jit(solution)/shard_map/ppermute | solution.py:144
  317.4 10.1 %collective-permute-done.2 = bf16[2560,80]{0,1:T(8,128)(2,1)S(1)} collective-permute-done((bf16[2560,80]{0,1:T(8,128)(2,1)S(1)}, bf16[2560,80]{0,1:T(8,128)(2,1)S(1)}, u32[]{:S(2)}, u32[]{:S(2)}) %collective-permute-start.2) | collective-permute-done | bytes 409632 | tf_op jit(solution)/shard_map/ppermute | solution.py:144
  327.5 10.1 %collective-permute-done.3 = bf16[2560,80]{0,1:T(8,128)(2,1)S(1)} collective-permute-done((bf16[2560,80]{0,1:T(8,128)(2,1)S(1)}, bf16[2560,80]{0,1:T(8,128)(2,1)S(1)}, u32[]{:S(2)}, u32[]{:S(2)}) %collective-permute-start.3) | collective-permute-done | bytes 409632 | tf_op jit(solution)/shard_map/ppermute | solution.py:144
  337.5 10.1 %collective-permute-done.4 = bf16[2560,80]{0,1:T(8,128)(2,1)S(1)} collective-permute-done((bf16[2560,80]{0,1:T(8,128)(2,1)S(1)}, bf16[2560,80]{0,1:T(8,128)(2,1)S(1)}, u32[]{:S(2)}, u32[]{:S(2)}) %collective-permute-start.4) | collective-permute-done | bytes 409632 | tf_op jit(solution)/shard_map/ppermute | solution.py:144
  347.6 10.1 %collective-permute-done.5 = bf16[2560,80]{0,1:T(8,128)(2,1)S(1)} collective-permute-done((bf16[2560,80]{0,1:T(8,128)(2,1)S(1)}, bf16[2560,80]{0,1:T(8,128)(2,1)S(1)}, u32[]{:S(2)}, u32[]{:S(2)}) %collective-permute-start.5) | collective-permute-done | bytes 409632 | tf_op jit(solution)/shard_map/ppermute | solution.py:144
  357.7 10.1 %collective-permute-done.6 = bf16[2560,80]{0,1:T(8,128)(2,1)S(1)} collective-permute-done((bf16[2560,80]{0,1:T(8,128)(2,1)S(1)}, bf16[2560,80]{0,1:T(8,128)(2,1)S(1)}, u32[]{:S(2)}, u32[]{:S(2)}) %collective-permute-start.6) | collective-permute-done | bytes 409632 | tf_op jit(solution)/shard_map/ppermute | solution.py:144
  367.8 10.1 %collective-permute-done.7 = bf16[2560,80]{0,1:T(8,128)(2,1)S(1)} collective-permute-done((bf16[2560,80]{0,1:T(8,128)(2,1)S(1)}, bf16[2560,80]{0,1:T(8,128)(2,1)S(1)}, u32[]{:S(2)}, u32[]{:S(2)}) %collective-permute-start.7) | collective-permute-done | bytes 409632 | tf_op jit(solution)/shard_map/ppermute | solution.py:144
  378.6 10.1 %collective-permute-done.8 = bf16[2560,80]{0,1:T(8,128)(2,1)S(1)} collective-permute-done((bf16[2560,80]{0,1:T(8,128)(2,1)S(1)}, bf16[2560,80]{0,1:T(8,128)(2,1)S(1)}, u32[]{:S(2)}, u32[]{:S(2)}) %collective-permute-start.8) | collective-permute-done | bytes 409632 | tf_op jit(solution)/shard_map/ppermute | solution.py:144
  389.5 10.2 %collective-permute-done.9 = bf16[2560,80]{0,1:T(8,128)(2,1)} collective-permute-done((bf16[2560,80]{0,1:T(8,128)(2,1)S(1)}, bf16[2560,80]{0,1:T(8,128)(2,1)}, u32[]{:S(2)}, u32[]{:S(2)}) %collective-permute-start.9) | collective-permute-done | bytes 409632 | tf_op jit(solution)/shard_map/ppermute | solution.py:144
  399.7 10.3 %collective-permute-done.10 = bf16[2560,80]{0,1:T(8,128)(2,1)} collective-permute-done((bf16[2560,80]{0,1:T(8,128)(2,1)}, bf16[2560,80]{0,1:T(8,128)(2,1)}, u32[]{:S(2)}, u32[]{:S(2)}) %collective-permute-start.10) | collective-permute-done | bytes 409632 | tf_op jit(solution)/shard_map/ppermute | solution.py:144
  410.0 19.0 %collective-permute-done.11 = bf16[2560,80]{0,1:T(8,128)(2,1)S(1)} collective-permute-done((bf16[2560,80]{0,1:T(8,128)(2,1)}, bf16[2560,80]{0,1:T(8,128)(2,1)S(1)}, u32[]{:S(2)}, u32[]{:S(2)}) %collective-permute-start.11) | collective-permute-done | bytes 409632 | tf_op jit(solution)/shard_map/ppermute | solution.py:144
  429.8 10.2 %collective-permute-done.12 = bf16[2560,80]{0,1:T(8,128)(2,1)S(1)} collective-permute-done((bf16[2560,80]{0,1:T(8,128)(2,1)S(1)}, bf16[2560,80]{0,1:T(8,128)(2,1)S(1)}, u32[]{:S(2)}, u32[]{:S(2)}) %collective-permute-start.12) | collective-permute-done | bytes 409632 | tf_op jit(solution)/shard_map/ppermute | solution.py:144
  440.8 19.0 %collective-permute-done.13 = bf16[2560,80]{0,1:T(8,128)(2,1)S(1)} collective-permute-done((bf16[2560,80]{0,1:T(8,128)(2,1)S(1)}, bf16[2560,80]{0,1:T(8,128)(2,1)S(1)}, u32[]{:S(2)}, u32[]{:S(2)}) %collective-permute-start.13) | collective-permute-done | bytes 409632 | tf_op jit(solution)/shard_map/ppermute | solution.py:144
  460.5 16.3 %collective-permute-done.14 = bf16[2560,80]{0,1:T(8,128)(2,1)} collective-permute-done((bf16[2560,80]{0,1:T(8,128)(2,1)S(1)}, bf16[2560,80]{0,1:T(8,128)(2,1)}, u32[]{:S(2)}, u32[]{:S(2)}) %collective-permute-start.14) | collective-permute-done | bytes 409632 | tf_op jit(solution)/shard_map/ppermute | solution.py:144
  476.8 10.4 %collective-permute-done.15 = bf16[2560,80]{0,1:T(8,128)(2,1)} collective-permute-done((bf16[2560,80]{0,1:T(8,128)(2,1)}, bf16[2560,80]{0,1:T(8,128)(2,1)}, u32[]{:S(2)}, u32[]{:S(2)}) %collective-permute-start.15) | collective-permute-done | bytes 409632 | tf_op jit(solution)/shard_map/ppermute | solution.py:144
  534.5 25.9 %all-gather.16.cloned.1.call-done = bf16[1024,1280]{1,0:T(8,128)(2,1)} async-done(((bf16[512,1280]{1,0:T(8,128)(2,1)}), bf16[1024,1280]{1,0:T(8,128)(2,1)}) %all-gather.16.cloned.1.call-update) | async-done | bytes 2621456 | tf_op jit(solution)/shard_map/all_gather | solution.py:131
  560.4 39.5 %fusion.88 = bf16[1024,1280]{1,0:T(8,128)(2,1)} fusion(bf16[2560,2560]{0,1:T(8,128)(2,1)} %constant_dynamic-update-slice_fusion, s32[]{:T(128)S(6)} %select_n.19, bf16[1024,1280]{1,0:T(8,128)(2,1)} %all-gather.16.cloned.1.call-done, bf16[1280,2560]{1,0:T(8,128)(2,1)} %all-gather.12.cloned.1.call-done), kind=kOutput, calls=%fused_computation.106 | convolution fusion | flops 13593477120 | bytes 18350084 | tf_op jit(solution)/shard_map/dot_general | solution.py:62
  600.0 37.8 %reduce-scatter.5.cloned.1.call-done = bf16[512,1280]{1,0:T(8,128)(2,1)} async-done(((bf16[1024,1280]{1,0:T(8,128)(2,1)}), bf16[512,1280]{1,0:T(8,128)(2,1)}) %reduce-scatter.5.cloned.1.call-update) | async-done | bytes 1310736 | tf_op jit(solution)/shard_map/reduce_scatter | solution.py:149
  (158 shorter events, 122.0 us)
Async XLA Ops:
  6.5 123.0 %copy-start = (bf16[3,3,256,512]{3,2,1,0:T(8,128)(2,1)S(1)}, bf16[3,3,256,512]{3,2,1,0:T(8,128)(2,1)}, u32[]{:S(2)}) copy-start(bf16[3,3,256,512]{3,2,1,0:T(8,128)(2,1)} %param.20) | copy-start | bytes 7077892
  6.5 169.7 %all-gather.14.cloned.1.call-start = ((), (), s32[]{:S(2)}) async-start(), calls=%async_computation.7 | async-start | bytes 3932160 | tf_op jit(solution)/shard_map/all_gather | solution.py:103
  7.5 6.6 %collective-permute-start = (bf16[1,3,15,512]{3,2,1,0:T(8,128)(2,1)S(1)}, bf16[1,3,15,512]{3,2,1,0:T(8,128)(2,1)S(1)}, u32[]{:S(2)}, u32[]{:S(2)}) collective-permute-start(bf16[1,3,15,512]{3,2,1,0:T(8,128)(2,1)S(1)} %slice.12), channel_id=1, source_target_pairs={{0,1},{2,3},{4,5},{6,7},{8,9},{10,11},{12,13},{14,15},{16,17},{18,... | collective-permute-start | bytes 138248 | tf_op jit(solution)/shard_map/ppermute | solution.py:12
  135.0 105.8 %copy-start.20 = (f32[1280]{0:T(1024)S(1)}, f32[1280]{0:T(1024)}, u32[]{:S(2)}) copy-start(f32[1280]{0:T(1024)} %param.22) | copy-start | bytes 15364
  135.0 97.6 %all-gather.8.cloned.1.call-start = ((), (), s32[]{:S(2)}) async-start(), calls=%async_computation.2 | async-start | bytes 5222400 | tf_op jit(solution)/shard_map/all_gather | solution.py:93
  135.8 165.8 %all-gather.10.cloned.1.call-start = ((), (), s32[]{:S(2)}) async-start(), calls=%async_computation.3 | async-start | bytes 1740800 | tf_op jit(solution)/shard_map/all_gather | solution.py:94
  136.5 382.7 %reduce-scatter.3.cloned.1.call-start = ((), (), s32[]{:S(2)}) async-start(), calls=%async_computation.4 | async-start | bytes 3932160 | tf_op jit(solution)/shard_map/reduce_scatter | solution.py:113
  307.2 227.3 %all-gather.12.cloned.1.call-start = ((), (), s32[]{:S(2)}) async-start(), calls=%async_computation.5 | async-start | bytes 6963200 | tf_op jit(solution)/shard_map/all_gather | solution.py:138
  307.3 10.1 %collective-permute-start.1 = (bf16[2560,80]{0,1:T(8,128)(2,1)S(1)}, bf16[2560,80]{0,1:T(8,128)(2,1)S(1)}, u32[]{:S(2)}, u32[]{:S(2)}) collective-permute-start(bf16[2560,80]{0,1:T(8,128)(2,1)S(1)} %copy-done.3), channel_id=1, source_target_pairs={{0,2},{2,4},{4,6},{6,8},{8,10},{10,12},{12,14},{14,16},{16,18},{18... | collective-permute-start | bytes 1228808 | tf_op jit(solution)/shard_map/ppermute | solution.py:144
  317.4 10.1 %collective-permute-start.2 = (bf16[2560,80]{0,1:T(8,128)(2,1)S(1)}, bf16[2560,80]{0,1:T(8,128)(2,1)S(1)}, u32[]{:S(2)}, u32[]{:S(2)}) collective-permute-start(bf16[2560,80]{0,1:T(8,128)(2,1)S(1)} %collective-permute-done.1), channel_id=1, source_target_pairs={{0,2},{2,4},{4,6},{6,8},{8,10},{10,12},{12,14},{14,16},{16,18},{18... | collective-permute-start | bytes 1228808 | tf_op jit(solution)/shard_map/ppermute | solution.py:144
  327.5 10.1 %collective-permute-start.3 = (bf16[2560,80]{0,1:T(8,128)(2,1)S(1)}, bf16[2560,80]{0,1:T(8,128)(2,1)S(1)}, u32[]{:S(2)}, u32[]{:S(2)}) collective-permute-start(bf16[2560,80]{0,1:T(8,128)(2,1)S(1)} %collective-permute-done.2), channel_id=1, source_target_pairs={{0,2},{2,4},{4,6},{6,8},{8,10},{10,12},{12,14},{14,16},{16,18},{18... | collective-permute-start | bytes 1228808 | tf_op jit(solution)/shard_map/ppermute | solution.py:144
  337.5 10.1 %collective-permute-start.4 = (bf16[2560,80]{0,1:T(8,128)(2,1)S(1)}, bf16[2560,80]{0,1:T(8,128)(2,1)S(1)}, u32[]{:S(2)}, u32[]{:S(2)}) collective-permute-start(bf16[2560,80]{0,1:T(8,128)(2,1)S(1)} %collective-permute-done.3), channel_id=1, source_target_pairs={{0,2},{2,4},{4,6},{6,8},{8,10},{10,12},{12,14},{14,16},{16,18},{18... | collective-permute-start | bytes 1228808 | tf_op jit(solution)/shard_map/ppermute | solution.py:144
  347.6 170.8 %copy-start.4 = (bf16[2560,80]{0,1:T(8,128)(2,1)}, bf16[2560,80]{0,1:T(8,128)(2,1)S(1)}, u32[]{:S(2)}) copy-start(bf16[2560,80]{0,1:T(8,128)(2,1)S(1)} %collective-permute-done.4) | copy-start | bytes 1228804
  347.6 10.1 %collective-permute-start.5 = (bf16[2560,80]{0,1:T(8,128)(2,1)S(1)}, bf16[2560,80]{0,1:T(8,128)(2,1)S(1)}, u32[]{:S(2)}, u32[]{:S(2)}) collective-permute-start(bf16[2560,80]{0,1:T(8,128)(2,1)S(1)} %collective-permute-done.4), channel_id=1, source_target_pairs={{0,2},{2,4},{4,6},{6,8},{8,10},{10,12},{12,14},{14,16},{16,18},{18... | collective-permute-start | bytes 1228808 | tf_op jit(solution)/shard_map/ppermute | solution.py:144
  357.7 160.7 %copy-start.5 = (bf16[2560,80]{0,1:T(8,128)(2,1)}, bf16[2560,80]{0,1:T(8,128)(2,1)S(1)}, u32[]{:S(2)}) copy-start(bf16[2560,80]{0,1:T(8,128)(2,1)S(1)} %collective-permute-done.5) | copy-start | bytes 1228804
  357.7 10.1 %collective-permute-start.6 = (bf16[2560,80]{0,1:T(8,128)(2,1)S(1)}, bf16[2560,80]{0,1:T(8,128)(2,1)S(1)}, u32[]{:S(2)}, u32[]{:S(2)}) collective-permute-start(bf16[2560,80]{0,1:T(8,128)(2,1)S(1)} %collective-permute-done.5), channel_id=1, source_target_pairs={{0,2},{2,4},{4,6},{6,8},{8,10},{10,12},{12,14},{14,16},{16,18},{18... | collective-permute-start | bytes 1228808 | tf_op jit(solution)/shard_map/ppermute | solution.py:144
  367.8 150.7 %copy-start.6 = (bf16[2560,80]{0,1:T(8,128)(2,1)}, bf16[2560,80]{0,1:T(8,128)(2,1)S(1)}, u32[]{:S(2)}) copy-start(bf16[2560,80]{0,1:T(8,128)(2,1)S(1)} %collective-permute-done.6) | copy-start | bytes 1228804
  367.8 10.1 %collective-permute-start.7 = (bf16[2560,80]{0,1:T(8,128)(2,1)S(1)}, bf16[2560,80]{0,1:T(8,128)(2,1)S(1)}, u32[]{:S(2)}, u32[]{:S(2)}) collective-permute-start(bf16[2560,80]{0,1:T(8,128)(2,1)S(1)} %collective-permute-done.6), channel_id=1, source_target_pairs={{0,2},{2,4},{4,6},{6,8},{8,10},{10,12},{12,14},{14,16},{16,18},{18... | collective-permute-start | bytes 1228808 | tf_op jit(solution)/shard_map/ppermute | solution.py:144
  378.6 10.1 %collective-permute-start.8 = (bf16[2560,80]{0,1:T(8,128)(2,1)S(1)}, bf16[2560,80]{0,1:T(8,128)(2,1)S(1)}, u32[]{:S(2)}, u32[]{:S(2)}) collective-permute-start(bf16[2560,80]{0,1:T(8,128)(2,1)S(1)} %collective-permute-done.7), channel_id=1, source_target_pairs={{0,2},{2,4},{4,6},{6,8},{8,10},{10,12},{12,14},{14,16},{16,18},{18... | collective-permute-start | bytes 1228808 | tf_op jit(solution)/shard_map/ppermute | solution.py:144
  389.5 10.2 %collective-permute-start.9 = (bf16[2560,80]{0,1:T(8,128)(2,1)S(1)}, bf16[2560,80]{0,1:T(8,128)(2,1)}, u32[]{:S(2)}, u32[]{:S(2)}) collective-permute-start(bf16[2560,80]{0,1:T(8,128)(2,1)S(1)} %collective-permute-done.8), channel_id=1, source_target_pairs={{0,2},{2,4},{4,6},{6,8},{8,10},{10,12},{12,14},{14,16},{16,18},{18... | collective-permute-start | bytes 1228808 | tf_op jit(solution)/shard_map/ppermute | solution.py:144
  399.6 10.4 %collective-permute-start.10 = (bf16[2560,80]{0,1:T(8,128)(2,1)}, bf16[2560,80]{0,1:T(8,128)(2,1)}, u32[]{:S(2)}, u32[]{:S(2)}) collective-permute-start(bf16[2560,80]{0,1:T(8,128)(2,1)} %collective-permute-done.9), channel_id=1, source_target_pairs={{0,2},{2,4},{4,6},{6,8},{8,10},{10,12},{12,14},{14,16},{16,18},{18... | collective-permute-start | bytes 1228808 | tf_op jit(solution)/shard_map/ppermute | solution.py:144
  399.7 160.7 %all-gather.16.cloned.1.call-start = ((), (), s32[]{:S(2)}) async-start(), calls=%async_computation.8 | async-start | bytes 3932160 | tf_op jit(solution)/shard_map/all_gather | solution.py:131
  410.0 19.0 %collective-permute-start.11 = (bf16[2560,80]{0,1:T(8,128)(2,1)}, bf16[2560,80]{0,1:T(8,128)(2,1)S(1)}, u32[]{:S(2)}, u32[]{:S(2)}) collective-permute-start(bf16[2560,80]{0,1:T(8,128)(2,1)} %collective-permute-done.10), channel_id=1, source_target_pairs={{0,2},{2,4},{4,6},{6,8},{8,10},{10,12},{12,14},{14,16},{16,18},{18... | collective-permute-start | bytes 1228808 | tf_op jit(solution)/shard_map/ppermute | solution.py:144
  429.8 10.2 %collective-permute-start.12 = (bf16[2560,80]{0,1:T(8,128)(2,1)S(1)}, bf16[2560,80]{0,1:T(8,128)(2,1)S(1)}, u32[]{:S(2)}, u32[]{:S(2)}) collective-permute-start(bf16[2560,80]{0,1:T(8,128)(2,1)S(1)} %collective-permute-done.11), channel_id=1, source_target_pairs={{0,2},{2,4},{4,6},{6,8},{8,10},{10,12},{12,14},{14,16},{16,18},{18... | collective-permute-start | bytes 1228808 | tf_op jit(solution)/shard_map/ppermute | solution.py:144
  440.8 19.0 %collective-permute-start.13 = (bf16[2560,80]{0,1:T(8,128)(2,1)S(1)}, bf16[2560,80]{0,1:T(8,128)(2,1)S(1)}, u32[]{:S(2)}, u32[]{:S(2)}) collective-permute-start(bf16[2560,80]{0,1:T(8,128)(2,1)S(1)} %collective-permute-done.12), channel_id=1, source_target_pairs={{0,2},{2,4},{4,6},{6,8},{8,10},{10,12},{12,14},{14,16},{16,18},{18... | collective-permute-start | bytes 1228808 | tf_op jit(solution)/shard_map/ppermute | solution.py:144
  460.5 16.3 %collective-permute-start.14 = (bf16[2560,80]{0,1:T(8,128)(2,1)S(1)}, bf16[2560,80]{0,1:T(8,128)(2,1)}, u32[]{:S(2)}, u32[]{:S(2)}) collective-permute-start(bf16[2560,80]{0,1:T(8,128)(2,1)S(1)} %collective-permute-done.13), channel_id=1, source_target_pairs={{0,2},{2,4},{4,6},{6,8},{8,10},{10,12},{12,14},{14,16},{16,18},{18... | collective-permute-start | bytes 1228808 | tf_op jit(solution)/shard_map/ppermute | solution.py:144
  476.8 10.4 %collective-permute-start.15 = (bf16[2560,80]{0,1:T(8,128)(2,1)}, bf16[2560,80]{0,1:T(8,128)(2,1)}, u32[]{:S(2)}, u32[]{:S(2)}) collective-permute-start(bf16[2560,80]{0,1:T(8,128)(2,1)} %collective-permute-done.14), channel_id=1, source_target_pairs={{0,2},{2,4},{4,6},{6,8},{8,10},{10,12},{12,14},{14,16},{16,18},{18... | collective-permute-start | bytes 1228808 | tf_op jit(solution)/shard_map/ppermute | solution.py:144
  476.8 36.5 %copy-start.13 = (bf16[2560,80]{0,1:T(8,128)(2,1)S(1)}, bf16[2560,80]{0,1:T(8,128)(2,1)}, u32[]{:S(2)}) copy-start(bf16[2560,80]{0,1:T(8,128)(2,1)} %copy-done.12) | copy-start | bytes 1228804
  476.8 37.3 %copy-start.11 = (bf16[2560,80]{0,1:T(8,128)(2,1)S(1)}, bf16[2560,80]{0,1:T(8,128)(2,1)}, u32[]{:S(2)}) copy-start(bf16[2560,80]{0,1:T(8,128)(2,1)} %copy-done.10) | copy-start | bytes 1228804
  476.8 41.6 %copy-start.9 = (bf16[2560,80]{0,1:T(8,128)(2,1)S(1)}, bf16[2560,80]{0,1:T(8,128)(2,1)}, u32[]{:S(2)}) copy-start(bf16[2560,80]{0,1:T(8,128)(2,1)} %copy-done.8) | copy-start | bytes 1228804
  524.0 113.8 %reduce-scatter.5.cloned.1.call-start = ((), (), s32[]{:S(2)}) async-start(), calls=%async_computation.6 | async-start | bytes 3932160 | tf_op jit(solution)/shard_map/reduce_scatter | solution.py:149
  560.4 80.4 %copy-start.1 = (bf16[3,3,256,512]{3,2,1,0:T(8,128)(2,1)S(1)}, bf16[3,3,256,512]{3,2,1,0:T(8,128)(2,1)}, u32[]{:S(2)}) copy-start(bf16[3,3,256,512]{3,2,1,0:T(8,128)(2,1)} %param.20) | copy-start | bytes 7077892
  (13 other events, 146.6 us)
Sparse Core Ops, SparseCore 0:
  135.1 41.0 all-gather.13
  178.5 54.1 all-gather.7
  234.8 38.4 all-gather.9
  307.3 36.3 reduce-scatter.2
  399.8 72.4 all-gather.11
  524.2 36.2 all-gather.15
  600.1 37.6 reduce-scatter.4
